TPU v7x, 16 devices: a 4x2x1 block of a 4x4x8 slice. The times are simulated.
16 devices in a mesh: dp: 2 (over y, z), ep: 8 (over x, core).
Axes of the slice: x: 4, y: 2, z: 1, core: 2. Of those that a mesh axis runs over, the one named last changes fastest.
The devices are a block of a 4x4x8 slice.
Arguments:
- x: bfloat16 [2, 8, 256, 2048], P('dp', 'ep'), parts along dimension 0
- expert: int32 [2, 8, 256, 2], P('dp', 'ep'), parts along dimension 0
- slot: int32 [2, 8, 256, 2], P('dp', 'ep'), parts along dimension 0
- gate: float32 [2, 8, 256, 2], P('dp', 'ep'), parts along dimension 0
- w_gate: bfloat16 [8, 2048, 5632], P('ep')
- w_up: bfloat16 [8, 2048, 5632], P('ep')
- w_down: bfloat16 [8, 5632, 2048], P('ep')
Outputs:
- y: bfloat16 [2, 8, 256, 2048], P('dp', 'ep'), parts along dimension 0
There are 2 independent parts. A program takes and returns all parts, laid end to end along the dimension named above; an argument that names none is the same for every part.
All inputs are finite; a program needn't handle non-finite values.
Results may differ from a plain program's by a relative error of at most 0.009.
Values are sent between devices in bfloat16 or wider.
A program may use at most 768 MiB of HBM per device.

v0:
```python
import jax
import jax.numpy as jnp
from jax import lax
from jax.sharding import NamedSharding, PartitionSpec as P


def einsum(form, a, b):
    return jnp.einsum(form, a.astype(jnp.float32), b.astype(jnp.float32))


def solution(mesh):
    def placed(v, *spec):
        return lax.with_sharding_constraint(v, NamedSharding(mesh, P(*spec)))

    def step(x, expert, slot, gate, w_gate, w_up, w_down):
        experts, (tokens, top) = w_gate.shape[0], expert.shape[2:]
        slots = 5 * tokens * top // (4 * experts)
        to_expert = jax.nn.one_hot(expert, experts, dtype=jnp.bfloat16)
        to_slot = jax.nn.one_hot(slot, slots, dtype=jnp.bfloat16)
        weighted = to_expert * gate[..., None].astype(jnp.bfloat16)
        dispatch = einsum("abtke,abtkc->abtec", to_expert, to_slot).astype(jnp.bfloat16)
        combine = einsum("abtke,abtkc->abtec", weighted, to_slot).astype(jnp.bfloat16)
        z = einsum("abtec,abtd->aebcd", dispatch, x).astype(jnp.bfloat16)
        z = placed(z, "dp", None, "ep", None, None)
        z = placed(z, "dp", "ep", None, None, None)
        h = jax.nn.silu(einsum("aebcd,edf->aebcf", z, w_gate))
        h = (h * einsum("aebcd,edf->aebcf", z, w_up)).astype(jnp.bfloat16)
        out = einsum("aebcf,efd->aebcd", h, w_down).astype(jnp.bfloat16)
        out = placed(out, "dp", "ep", None, None, None)
        out = placed(out, "dp", None, "ep", None, None)
        y = einsum("abtec,aebcd->abtd", combine, out)
        return y.astype(jnp.bfloat16)

    return step
```

profile of v0, /device:TPU:113, one launch (start us, length us, event | category | flops | bytes accessed | tf_op | source)
XLA Modules:
  0.0 153.3 jit_solution(17184150376553035987)
XLA Ops:
  0.0 0.0 copy-start
  0.0 0.9 copy.3
  0.9 0.8 copy.5
  1.7 1.8 %fusion.39 = bf16[256,8,80]{2,1,0:T(8,128)(2,1)S(1)} fusion(s32[256,2]{1,0:T(8,128)S(1)} %copy.5, s32[256,2]{1,0:T(8,128)S(1)} %copy.3), kind=kOutput, calls=%fused_computation.25 | convolution fusion | flops 700416 | bytes 331776 | tf_op jit(solution)/abtke,abtkc->abtec/dot_general | solution.py:8
  3.5 0.3 copy.9
  3.8 0.0 copy-done
  3.8 0.8 fusion.22
  4.7 37.6 %all-to-all.4 = bf16[1,8,1,1,80,2048]{5,4,3,2,0,1:T(8,128)(2,1)S(1)} all-to-all(bf16[1,8,1,1,80,2048]{5,4,3,2,0,1:T(8,128)(2,1)S(1)} %fusion.22), channel_id=1, replica_groups=mesh['dp'=2,'ep'=8] {'ep'}, dimensions={1} | all-to-all | bytes 5242880 | tf_op jit(solution)/sharding_constraint;jit(solution)/sharding_constraint | solution.py:13
  42.3 0.0 copy-start.2
  42.3 1.5 copy-done.2
  43.8 22.4 %fusion.4 = f32[8,80,5632]{2,1,0:T(8,128)} fusion(bf16[1,2048,5632]{2,1,0:T(8,128)(2,1)} %param.4, bf16[1,8,1,1,80,2048]{5,4,3,2,0,1:T(8,128)(2,1)S(1)} %all-to-all.4), kind=kOutput, calls=%fused_computation.4 | convolution fusion | flops 14763950080 | bytes 40108032 | tf_op jit(solution)/aebcd,edf->aebcf/dot_general | solution.py:8
  66.2 24.5 %fusion.12.clone.8 = bf16[8,80,5632]{2,1,0:T(8,128)(2,1)} fusion(bf16[1,2048,5632]{2,1,0:T(8,128)(2,1)} %param.5, f32[8,80,5632]{2,1,0:T(8,128)} %fusion.4, bf16[1,8,1,1,80,2048]{5,4,3,2,0,1:T(8,128)(2,1)} %copy-done.2), kind=kOutput, calls=%fused_computation.13.clone.clone.clone.clone.clone.clone.clone.1 | convolution fusion | flops 14785576960 | bytes 47316992 | tf_op jit(solution)/aebcd,edf->aebcf/dot_general | solution.py:8
  90.8 0.0 copy-start.3
  90.8 0.0 copy-start.1
  90.8 21.5 %fusion.23 = bf16[1,1,8,1,80,2048]{5,4,3,1,0,2:T(8,128)(2,1)} fusion(bf16[1,5632,2048]{2,1,0:T(8,128)(2,1)} %param.6, bf16[8,80,5632]{2,1,0:T(8,128)(2,1)} %fusion.12.clone.8), kind=kOutput, calls=%fused_computation.17 | convolution fusion | flops 14765260800 | bytes 32899072 | tf_op jit(solution)/aebcf,efd->aebcd/dot_general | solution.py:8
  112.3 5.4 %all-to-all-start.1 = ((bf16[1,1,8,1,80,2048]{5,4,3,1,0,2:T(8,128)(2,1)}), bf16[1,1,8,1,80,2048]{5,4,3,1,0,2:T(8,128)(2,1)}, u32[]{:S(2)}, u32[]{:S(2)}) async-start(bf16[1,1,8,1,80,2048]{5,4,3,1,0,2:T(8,128)(2,1)} %fusion.23), calls=%async_computation.1 | async-start | bytes 5242880 | tf_op jit(solution)/sharding_constraint;jit(solution)/sharding_constraint | solution.py:13
  117.7 0.0 copy-done.3
  117.7 0.1 copy.4
  117.9 2.2 %fusion.42 = bf16[256,8,80]{2,1,0:T(8,128)(2,1)S(1)} fusion(s32[256,2]{1,0:T(8,128)S(1)} %copy.5, s32[256,2]{1,0:T(8,128)S(1)} %copy.3, bf16[256,2]{1,0:T(8,128)(2,1)S(1)} %copy.4), kind=kOutput, calls=%fused_computation.28 | convolution fusion | flops 704512 | bytes 332800 | tf_op jit(solution)/abtke,abtkc->abtec/dot_general | solution.py:8
  120.1 0.3 copy.8
  120.4 29.1 %all-to-all-done.1 = bf16[1,1,8,1,80,2048]{5,4,3,1,0,2:T(8,128)(2,1)} async-done(((bf16[1,1,8,1,80,2048]{5,4,3,1,0,2:T(8,128)(2,1)}), bf16[1,1,8,1,80,2048]{5,4,3,1,0,2:T(8,128)(2,1)}, u32[]{:S(2)}, u32[]{:S(2)}) %all-to-all-start.1) | async-done | bytes 2621472 | tf_op jit(solution)/sharding_constraint;jit(solution)/sharding_constraint | solution.py:13
  149.5 3.7 %fusion.35 = bf16[1,1,256,2048]{3,2,1,0:T(8,128)(2,1)} fusion(bf16[1,1,8,1,80,2048]{5,4,3,1,0,2:T(8,128)(2,1)} %all-to-all-done.1, bf16[256,8,80]{0,2,1:T(8,128)(2,1)S(1)} %copy.8), kind=kOutput, calls=%fused_computation.23 | convolution fusion | flops 671612928 | bytes 3997696 | tf_op jit(solution)/abtec,aebcd->abtd/dot_general | solution.py:8
  153.3 0.0 copy-done.1
  (1 shorter events, 0.0 us)
Async XLA Ops:
  0.0 3.8 %copy-start = (bf16[1,1,256,2048]{3,2,1,0:T(8,128)(2,1)S(1)}, bf16[1,1,256,2048]{3,2,1,0:T(8,128)(2,1)}, u32[]{:S(2)}) copy-start(bf16[1,1,256,2048]{3,2,1,0:T(8,128)(2,1)} %param.3) | copy-start | bytes 3145732
  42.3 1.5 copy-start.2
  90.8 26.9 %copy-start.3 = (f32[1,1,256,2]{2,3,1,0:T(2,128)S(1)}, f32[1,1,256,2]{2,3,1,0:T(2,128)}, u32[]{:S(2)}) copy-start(f32[1,1,256,2]{2,3,1,0:T(2,128)} %param.1) | copy-start | bytes 6148
  90.8 62.5 %copy-start.1 = (bf16[1,1,256,2048]{3,2,1,0:T(8,128)(2,1)S(1)}, bf16[1,1,256,2048]{3,2,1,0:T(8,128)(2,1)}, u32[]{:S(2)}) copy-start(bf16[1,1,256,2048]{3,2,1,0:T(8,128)(2,1)} %param.3) | copy-start | bytes 3145732
  112.3 37.2 %all-to-all-start.1 = ((bf16[1,1,8,1,80,2048]{5,4,3,1,0,2:T(8,128)(2,1)}), bf16[1,1,8,1,80,2048]{5,4,3,1,0,2:T(8,128)(2,1)}, u32[]{:S(2)}, u32[]{:S(2)}) async-start(bf16[1,1,8,1,80,2048]{5,4,3,1,0,2:T(8,128)(2,1)} %fusion.23), calls=%async_computation.1 | async-start | bytes 5242880 | tf_op jit(solution)/sharding_constraint;jit(solution)/sharding_constraint | solution.py:13
where the time goes:
time: 154 us; the launch traced here: 153 us
  matrix products  77 us (50%)
  blocking collectives  37.6 us (24%)
  waiting for transfers between devices  29.1 us (19%)
  starting transfers between devices  5.43 us (4%)
  local copies, waits for them, and re-layouts  4.05 us (3%)
    dot_general x7, matrix products, einsum(): return jnp.einsum(form, a.astype(jnp.float32), b.astype(jnp.float32))  77 us
    another operation x1, blocking collectives, placed(): return lax.with_sharding_constraint(v, NamedSharding(mesh, P(*spec)))  37.6 us
    another operation x1, waiting for transfers between devices, placed(): return lax.with_sharding_constraint(v, NamedSharding(mesh, P(*spec)))  29.1 us
    another operation x1, starting transfers between devices, placed(): return lax.with_sharding_constraint(v, NamedSharding(mesh, P(*spec)))  5.43 us
    unnamed x10, local copies, waits for them, and re-layouts  3.24 us
  transfers between devices with their start and end apart: 1, of which 1 were waited for; matrix products, arithmetic and copies ran while one was open for 2% of the time, Pallas kernels for 0%

commit v1 on v0

v1 whole, which is shorter than its diff:
```python
import functools

import jax
import jax.numpy as jnp
from jax import lax
from jax.experimental import pallas as pl
from jax.experimental.pallas import tpu as pltpu
from jax.sharding import PartitionSpec as P

MESH = pl.DeviceIdType.MESH
F_TILE = 512
D_TILE = 256
RING = 4
AHEAD = 3
SPLITS = ((0, 16, 48, 80), (0, 32, 64, 80), (0, 32, 48, 80))
FLIP = (0, 2, 1)
f32, bf16 = jnp.float32, jnp.bfloat16


def dot(a, b):
    return jnp.dot(a, b, preferred_element_type=f32)


def kernel(
    n_ep, slots,
    x_hbm, ex_ref, sl_ref, gt_ref, wg_hbm, wu_hbm, wd_hbm, y_hbm,
    z, zs, h, wg, wu, wd, comb,
    x_sem, g_sem, u_sem, d_sem, y_sem, out_send, out_recv, back_send, back_recv, free,
):
    tokens, dim = x_hbm.shape[2:]
    ff = h.shape[1]
    n_f, n_d = ff // F_TILE, dim // (2 * D_TILE)
    rows = h.shape[0]
    wide = 2 * D_TILE
    me = lax.axis_index("ep")
    chips = n_ep // 2
    chip, core = me // 2, lax.rem(me, 2)

    def peer(cls, c):
        step = (chips // 2, 1, chips - 1)[cls]
        return lax.rem(chip + step, chips) * 2 + c

    sibling = chip * 2 + 1 - core

    def load_f(i):
        cols = pl.ds(pl.multiple_of(i * F_TILE, F_TILE), F_TILE)
        return (
            pltpu.make_async_copy(wg_hbm.at[0, :, cols], wg.at[i], g_sem.at[i]),
            pltpu.make_async_copy(wu_hbm.at[0, :, cols], wu.at[i], u_sem.at[i]),
        )

    def load_d(block, slot):
        cols = pl.ds(pl.multiple_of(block * D_TILE, D_TILE), D_TILE)
        return pltpu.make_async_copy(wd_hbm.at[0, :, cols], wd.at[slot], d_sem.at[slot])

    def column(b):
        return pl.ds(pl.multiple_of(b * D_TILE, D_TILE), D_TILE)

    def strip(b):
        return pl.ds(pl.multiple_of(b * tokens, tokens), tokens)

    def get_x(b):
        return pltpu.make_async_copy(
            x_hbm.at[0, 0, :, column(b)], wd.at[RING - 1, strip(b)], x_sem.at[b]
        )

    for b in range(dim // D_TILE):
        get_x(b).start()
    for i in range(AHEAD):
        for c in load_f(i):
            c.start()

    barrier = pltpu.get_barrier_semaphore()
    for k in range(1, n_ep):
        pl.semaphore_signal(
            barrier, inc=1, device_id={"ep": lax.rem(me + k, n_ep)}, device_id_type=MESH
        )

    order = [me, sibling] + [peer(cls, c) for cls in range(3) for c in range(2)]
    top = ex_ref.shape[0]
    expert, slot_of = ex_ref[...], sl_ref[...]
    rank = functools.reduce(
        lambda v, r: jnp.where(expert == order[r], r, v), range(1, n_ep), jnp.zeros_like(expert)
    )
    key = jnp.where(slot_of < slots, rank * slots + slot_of, -1)

    def hit(start, size, k):
        at = start + lax.broadcasted_iota(jnp.int32, (size, tokens), 0)
        return key[k : k + 1, :] == at

    for p in range(n_ep // 2):
        hits = [hit(p * rows, rows, k) for k in range(top)]
        any_hit = functools.reduce(jnp.logical_or, hits)
        h[:, p * tokens : (p + 1) * tokens] = jnp.where(any_hit, 1.0, 0.0).astype(bf16)
    for b in range(dim // D_TILE):
        get_x(b).wait()

    def dispatch(b, _):
        tile = wd[RING - 1, strip(b), :]
        for p in reversed(range(n_ep // 2)):
            out = dot(h[:, p * tokens : (p + 1) * tokens], tile).astype(bf16)
            if p == 0:
                z[0:slots, column(b)] = out[0:slots]
                zs[slots:rows, column(b)] = out[slots:rows]
            else:
                zs[p * rows : (p + 1) * rows, column(b)] = out
        return 0

    lax.fori_loop(0, dim // D_TILE, dispatch, 0)

    def unit(g, cls, c):
        return ((g - 1) * 3 + cls) * 2 + c

    last = 6 * (len(SPLITS[0]) - 1)

    def place(g, cls, c):
        sizes = [SPLITS[q][g] - SPLITS[q][g - 1] for q in range(3)]
        return g * rows + 2 * sum(sizes[:cls]) + c * sizes[cls], sizes[cls]

    def home(g, cls, c):
        return (2 + 2 * cls + c) * slots + SPLITS[FLIP[cls]][g - 1]

    def go(g, cls, c):
        there, n = place(g, FLIP[cls], core)
        there = pl.multiple_of(there, 16)
        return pltpu.make_async_remote_copy(
            src_ref=zs.at[pl.ds(home(g, cls, c), n)],
            dst_ref=z.at[pl.ds(there, n)],
            send_sem=out_send.at[unit(g, cls, c)],
            recv_sem=out_recv.at[unit(g, FLIP[cls], core)],
            device_id={"ep": peer(cls, c)},
            device_id_type=MESH,
        )

    def come(g, cls, c):
        here, n = place(g, cls, c)
        return pltpu.make_async_remote_copy(
            src_ref=zs.at[pl.ds(0, n)],
            dst_ref=z.at[pl.ds(here, n)],
            send_sem=out_send.at[unit(g, cls, c)],
            recv_sem=out_recv.at[unit(g, cls, c)],
            device_id={"ep": peer(cls, c)},
            device_id_type=MESH,
        )

    go_sib = pltpu.make_async_remote_copy(
        src_ref=zs.at[pl.ds(slots, slots)],
        dst_ref=z.at[pl.ds(slots, slots)],
        send_sem=out_send.at[last],
        recv_sem=out_recv.at[last],
        device_id={"ep": sibling},
        device_id_type=MESH,
    )
    passes = range(1, len(SPLITS[0]))
    peers = [(cls, c) for cls in range(3) for c in range(2)]
    near = [(1, 0), (2, 0), (1, 1), (2, 1), (0, 0), (0, 1)]

    pl.semaphore_wait(barrier, n_ep - 1)
    go_sib.start()
    for g in passes:
        for cls, c in near:
            go(g, cls, c).start()

    gates = gt_ref[...].astype(bf16).astype(f32)
    for start in range(0, n_ep * slots, 128):
        part = jnp.zeros((128, tokens), f32)
        for k in range(top):
            part = part + jnp.where(hit(start, 128, k), gates[k : k + 1, :], 0.0)
        comb[:, start : start + 128] = part.T.astype(bf16)

    def back(g, cls, c, j):
        here, n = place(g, cls, c)
        there = pl.multiple_of(
            (2 + 2 * FLIP[cls] + core) * slots + SPLITS[cls][g - 1], 16
        )
        cols = pl.ds(pl.multiple_of(j * wide, wide), wide)
        return pltpu.make_async_remote_copy(
            src_ref=z.at[pl.ds(here, n), cols],
            dst_ref=zs.at[pl.ds(there, n), cols],
            send_sem=back_send.at[unit(g, cls, c), j],
            recv_sem=back_recv.at[unit(g, FLIP[cls], core), j],
            device_id={"ep": peer(cls, c)},
            device_id_type=MESH,
        )

    def back_here(g, cls, c, j):
        here = home(g, cls, c)
        n = place(g, FLIP[cls], 0)[1]
        cols = pl.ds(pl.multiple_of(j * wide, wide), wide)
        return pltpu.make_async_remote_copy(
            src_ref=z.at[pl.ds(0, n), cols],
            dst_ref=zs.at[pl.ds(here, n), cols],
            send_sem=back_send.at[unit(g, cls, c), j],
            recv_sem=back_recv.at[unit(g, cls, c), j],
            device_id={"ep": peer(cls, c)},
            device_id_type=MESH,
        )

    def back_sib(j):
        cols = pl.ds(pl.multiple_of(j * wide, wide), wide)
        return pltpu.make_async_remote_copy(
            src_ref=z.at[pl.ds(slots, slots), cols],
            dst_ref=zs.at[pl.ds(slots, slots), cols],
            send_sem=back_send.at[last, j],
            recv_sem=back_recv.at[last, j],
            device_id={"ep": sibling},
            device_id_type=MESH,
        )

    n_pass = len(SPLITS[0])
    blocks = 2 * n_d

    for g in range(n_pass):
        first = g * rows
        if g == 0:
            go_sib.wait()
            pl.semaphore_signal(
                free.at[last], inc=1, device_id={"ep": sibling}, device_id_type=MESH
            )
        else:
            for cls, c in peers:
                come(g, cls, c).wait_recv()
                go(g, cls, c).wait_send()
                pl.semaphore_signal(
                    free.at[unit(g, FLIP[cls], core)],
                    inc=1,
                    device_id={"ep": peer(cls, c)},
                    device_id_type=MESH,
                )

        def gate_up(i, _):
            if g == 0:
                for c in load_f(i):
                    c.wait()

                @pl.when(i + AHEAD < n_f)
                def _():
                    for c in load_f(i + AHEAD):
                        c.start()

                @pl.when(jnp.logical_and(i + AHEAD >= n_f, i + AHEAD < n_f + RING))
                def _():
                    q = i + AHEAD - n_f
                    load_d(q, q).start()

            rows_in = z[first : first + rows, :]
            a = dot(rows_in, wg[i])
            b = dot(rows_in, wu[i])
            cols = pl.ds(pl.multiple_of(i * F_TILE, F_TILE), F_TILE)
            h[:, cols] = (a * jax.nn.sigmoid(a) * b).astype(bf16)
            return 0

        lax.fori_loop(0, n_f, gate_up, 0)
        if g == 0:
            for q in range(AHEAD, RING):
                load_d(q, q).start()

        def down(j, _):
            for s in range(2):
                q = 2 * j + s
                slot = lax.rem(q, RING)
                load_d(q, slot).wait()
            q0 = lax.rem(2 * j, RING)
            a = dot(h[...], wd[q0])
            b = dot(h[...], wd[q0 + 1])
            col = pl.multiple_of(j * wide, wide)
            z[first : first + rows, pl.ds(col, D_TILE)] = a.astype(bf16)
            z[first : first + rows, pl.ds(col + D_TILE, D_TILE)] = b.astype(bf16)
            if g == 0:
                zs[0:slots, pl.ds(col, D_TILE)] = a[0:slots].astype(bf16)
                zs[0:slots, pl.ds(col + D_TILE, D_TILE)] = b[0:slots].astype(bf16)

            def refill():
                for s in range(2):
                    q = 2 * j + s + RING
                    load_d(lax.rem(q, blocks), lax.rem(q, RING)).start()

            if g < n_pass - 1:
                refill()
            else:
                pl.when(2 * j + RING < blocks)(refill)
            if g == 0:
                back_sib(j).start()
            else:
                for cls, c in near:
                    back(g, cls, c, j).start()
            return 0

        if g == 0:
            pl.semaphore_wait(free.at[last], 1)
        else:
            for cls, c in peers:
                pl.semaphore_wait(free.at[unit(g, cls, c)], 1)
        lax.fori_loop(0, n_d, down, 0)

    def put(b):
        return pltpu.make_async_copy(
            wd.at[0, strip(b)], y_hbm.at[0, 0, :, column(b)], y_sem.at[b]
        )

    def combine(j, _):
        back_sib(j).wait()
        for g in passes:
            for cls, c in peers:
                back_here(g, cls, c, j).wait_recv()
                back(g, cls, c, j).wait_send()
        for s in range(2):
            b = 2 * j + s
            wd[0, strip(b), :] = dot(comb[...], zs[:, column(b)]).astype(bf16)
            put(b).start()
        return 0

    lax.fori_loop(0, n_d, combine, 0)
    for b in range(2 * n_d):
        put(b).wait()


def solution(mesh):
    n_ep = mesh.shape["ep"]

    def local(x, expert, slot, gate, w_gate, w_up, w_down):
        tokens, dim = x.shape[2:]
        top, ff = expert.shape[3], w_gate.shape[2]
        slots = 5 * tokens * top // (4 * n_ep)
        rows = 2 * slots
        n_d = dim // (2 * D_TILE)
        units = 6 * (len(SPLITS[0]) - 1) + 1
        dma = pltpu.SemaphoreType.DMA
        hbm = pl.BlockSpec(memory_space=pltpu.MemorySpace.HBM)
        vmem = pl.BlockSpec(memory_space=pltpu.VMEM)
        return pl.pallas_call(
            functools.partial(kernel, n_ep, slots),
            out_shape=jax.ShapeDtypeStruct(x.shape, x.dtype),
            in_specs=[hbm, vmem, vmem, vmem, hbm, hbm, hbm],
            out_specs=hbm,
            scratch_shapes=[
                pltpu.VMEM((n_ep * slots, dim), bf16),
                pltpu.VMEM((n_ep * slots, dim), bf16),
                pltpu.VMEM((rows, ff), bf16),
                pltpu.VMEM((ff // F_TILE, dim, F_TILE), bf16),
                pltpu.VMEM((ff // F_TILE, dim, F_TILE), bf16),
                pltpu.VMEM((RING, ff, D_TILE), bf16),
                pltpu.VMEM((tokens, n_ep * slots), bf16),
                dma((dim // D_TILE,)),
                dma((ff // F_TILE,)),
                dma((ff // F_TILE,)),
                dma((RING,)),
                dma((dim // D_TILE,)),
                dma((units,)),
                dma((units,)),
                dma((units, n_d)),
                dma((units, n_d)),
                pltpu.SemaphoreType.REGULAR((units,)),
            ],
            compiler_params=pltpu.CompilerParams(
                collective_id=0, has_side_effects=True, vmem_limit_bytes=67_043_328
            ),
        )(
            x,
            expert.reshape(tokens, top).T,
            slot.reshape(tokens, top).T,
            gate.reshape(tokens, top).T,
            w_gate,
            w_up,
            w_down,
        )

    act, wt = P("dp", "ep", None, None), P("ep", None, None)
    return jax.shard_map(
        local, mesh=mesh, in_specs=(act,) * 4 + (wt,) * 3, out_specs=act, check_vma=False
    )
```

time: 154 us -> 91.5 us (0.59)
  Pallas kernels: 0 us -> 88 us
  matrix products: 77 us -> 0 us
  blocking collectives: 37.6 us -> 0 us
  waiting for transfers between devices: 29.1 us -> 0 us
  starting transfers between devices: 5.43 us -> 0 us
  local copies, waits for them, and re-layouts: 4.05 us -> 2.3 us
    pallas_call x0 -> x1, Pallas kernels: none -> 88 us  [local(): pl.pallas_call(functools.partial(kernel, n_ep, slots), out_shape=jax.Shap...]
    dot_general x7 -> x0, matrix products: 77 us -> none  [einsum(): return jnp.einsum(form, a.astype(jnp.float32), b.astype(jnp.float32))]
    another operation x1 -> x0, blocking collectives: 37.6 us -> none  [placed(): return lax.with_sharding_constraint(v, NamedSharding(mesh, P(*spec)))]
    another operation x1 -> x0, waiting for transfers between devices: 29.1 us -> none  [placed(): return lax.with_sharding_constraint(v, NamedSharding(mesh, P(*spec)))]
    another operation x1 -> x0, starting transfers between devices: 5.43 us -> none  [placed(): return lax.with_sharding_constraint(v, NamedSharding(mesh, P(*spec)))]
    unnamed x10 -> x1, local copies, waits for them, and re-layouts: 3.24 us -> 2.3 us
  transfers between devices with their start and end apart: 1 -> 0, of which waited for: 1 -> 0; matrix products, arithmetic and copies ran while one was open for 2% -> 0% of each run, Pallas kernels for 0% -> 0%
where the time goes in v1:
time: 91.5 us; the launch traced here: 90.3 us
  Pallas kernels  88 us (96%)
  local copies, waits for them, and re-layouts  2.3 us (3%)
    pallas_call x1, Pallas kernels, local(): pl.pallas_call(functools.partial(kernel, n_ep, slots), out_shape=jax.Shap...  88 us
    unnamed x1, local copies, waits for them, and re-layouts  2.3 us

profile of v1, /device:TPU:113, one launch (start us, length us, event | category | flops | bytes accessed | tf_op | source)
XLA Modules:
  0.0 90.3 jit_solution(13385542993362457010)
XLA Ops:
  0.0 88.0 %shard_map.73 = bf16[1,1,256,2048]{3,2,1,0:T(8,128)(2,1)} custom-call(bf16[1,1,256,2048]{3,2,1,0:T(8,128)(2,1)} %x_hbm.1, s32[2,256]{1,0:T(2,128)} %bitcast.9, s32[2,256]{1,0:T(2,128)} %bitcast.10, f32[2,256]{1,0:T(2,128)} %bitcast.11, bf16[1,2048,5632]{2,1,0:T(8,128)(2,1)} %wg_hbm.1, bf16[1,2048,5632]{2,1,0:T(8,128)(2,1)} %wu_hbm.1, ...), custom_call_target="tpu_custom_call" | custom-call | tf_op jit(solution)/shard_map/pallas_call | solution.py:331
  88.0 2.3 %copy.9 = bf16[1,1,256,2048]{3,2,1,0:T(8,128)(2,1)} copy(bf16[1,1,256,2048]{3,2,1,0:T(8,128)(2,1)} %shard_map.73) | data formatting | bytes 2097152

commit v2 on v1

--- a/solution.py
+++ b/solution.py
@@ -10,7 +10,7 @@
 MESH = pl.DeviceIdType.MESH
 F_TILE = 512
 D_TILE = 256
-RING = 4
+RING = 3
 AHEAD = 3
 SPLITS = ((0, 16, 48, 80), (0, 32, 64, 80), (0, 32, 48, 80))
 FLIP = (0, 2, 1)
@@ -28,10 +28,10 @@
     x_sem, g_sem, u_sem, d_sem, y_sem, out_send, out_recv, back_send, back_recv, free,
 ):
     tokens, dim = x_hbm.shape[2:]
-    ff = h.shape[1]
-    n_f, n_d = ff // F_TILE, dim // (2 * D_TILE)
-    rows = h.shape[0]
-    wide = 2 * D_TILE
+    ff = h.shape[2]
+    n_f, n_d = ff // F_TILE, dim // D_TILE
+    rows = h.shape[1]
+    wide = D_TILE
     me = lax.axis_index("ep")
     chips = n_ep // 2
     chip, core = me // 2, lax.rem(me, 2)
@@ -91,14 +91,14 @@
     for p in range(n_ep // 2):
         hits = [hit(p * rows, rows, k) for k in range(top)]
         any_hit = functools.reduce(jnp.logical_or, hits)
-        h[:, p * tokens : (p + 1) * tokens] = jnp.where(any_hit, 1.0, 0.0).astype(bf16)
+        h[0, :, p * tokens : (p + 1) * tokens] = jnp.where(any_hit, 1.0, 0.0).astype(bf16)
     for b in range(dim // D_TILE):
         get_x(b).wait()
 
     def dispatch(b, _):
         tile = wd[RING - 1, strip(b), :]
         for p in reversed(range(n_ep // 2)):
-            out = dot(h[:, p * tokens : (p + 1) * tokens], tile).astype(bf16)
+            out = dot(h[0, :, p * tokens : (p + 1) * tokens], tile).astype(bf16)
             if p == 0:
                 z[0:slots, column(b)] = out[0:slots]
                 zs[slots:rows, column(b)] = out[slots:rows]
@@ -207,11 +207,7 @@
             device_id_type=MESH,
         )
 
-    n_pass = len(SPLITS[0])
-    blocks = 2 * n_d
-
-    for g in range(n_pass):
-        first = g * rows
+    def gather(g):
         if g == 0:
             go_sib.wait()
             pl.semaphore_signal(
@@ -228,6 +224,9 @@
                     device_id_type=MESH,
                 )
 
+    def expand(g, to):
+        gather(g)
+
         def gate_up(i, _):
             if g == 0:
                 for c in load_f(i):
@@ -238,60 +237,61 @@
                     for c in load_f(i + AHEAD):
                         c.start()
 
-                @pl.when(jnp.logical_and(i + AHEAD >= n_f, i + AHEAD < n_f + RING))
+                @pl.when(i + AHEAD >= n_f)
                 def _():
                     q = i + AHEAD - n_f
                     load_d(q, q).start()
 
-            rows_in = z[first : first + rows, :]
+            rows_in = z[g * rows : (g + 1) * rows, :]
             a = dot(rows_in, wg[i])
             b = dot(rows_in, wu[i])
             cols = pl.ds(pl.multiple_of(i * F_TILE, F_TILE), F_TILE)
-            h[:, cols] = (a * jax.nn.sigmoid(a) * b).astype(bf16)
+            h[to, :, cols] = (a * jax.nn.sigmoid(a) * b).astype(bf16)
             return 0
 
         lax.fori_loop(0, n_f, gate_up, 0)
-        if g == 0:
-            for q in range(AHEAD, RING):
-                load_d(q, q).start()
+
+    def contract(pair, start, more):
+        for g, _ in pair:
+            if g == 0:
+                pl.semaphore_wait(free.at[last], 1)
+            else:
+                for cls, c in peers:
+                    pl.semaphore_wait(free.at[unit(g, cls, c)], 1)
 
         def down(j, _):
-            for s in range(2):
-                q = 2 * j + s
-                slot = lax.rem(q, RING)
-                load_d(q, slot).wait()
-            q0 = lax.rem(2 * j, RING)
-            a = dot(h[...], wd[q0])
-            b = dot(h[...], wd[q0 + 1])
-            col = pl.multiple_of(j * wide, wide)
-            z[first : first + rows, pl.ds(col, D_TILE)] = a.astype(bf16)
-            z[first : first + rows, pl.ds(col + D_TILE, D_TILE)] = b.astype(bf16)
-            if g == 0:
-                zs[0:slots, pl.ds(col, D_TILE)] = a[0:slots].astype(bf16)
-                zs[0:slots, pl.ds(col + D_TILE, D_TILE)] = b[0:slots].astype(bf16)
+            q = start + j
+            slot = lax.rem(q, RING)
+            load_d(j, slot).wait()
+            outs = [dot(h[at], wd[slot]).astype(bf16) for _, at in pair]
+            for (g, _), out in zip(pair, outs):
+                z[g * rows : (g + 1) * rows, column(j)] = out
+                if g == 0:
+                    zs[0:slots, column(j)] = out[0:slots]
 
             def refill():
-                for s in range(2):
-                    q = 2 * j + s + RING
-                    load_d(lax.rem(q, blocks), lax.rem(q, RING)).start()
-
-            if g < n_pass - 1:
+                load_d(lax.rem(j + RING, n_d), slot).start()
+
+            if more:
                 refill()
             else:
-                pl.when(2 * j + RING < blocks)(refill)
-            if g == 0:
-                back_sib(j).start()
-            else:
-                for cls, c in near:
-                    back(g, cls, c, j).start()
+                pl.when(j + RING < n_d)(refill)
+            for g, _ in pair:
+                if g == 0:
+                    back_sib(j).start()
+                else:
+                    for cls, c in near:
+                        back(g, cls, c, j).start()
             return 0
 
-        if g == 0:
-            pl.semaphore_wait(free.at[last], 1)
-        else:
-            for cls, c in peers:
-                pl.semaphore_wait(free.at[unit(g, cls, c)], 1)
         lax.fori_loop(0, n_d, down, 0)
+
+    expand(0, 2)
+    expand(1, 0)
+    expand(2, 1)
+    contract(((1, 0), (2, 1)), 0, True)
+    expand(3, 0)
+    contract(((3, 0), (0, 2)), n_d, False)
 
     def put(b):
         return pltpu.make_async_copy(
@@ -304,14 +304,12 @@
             for cls, c in peers:
                 back_here(g, cls, c, j).wait_recv()
                 back(g, cls, c, j).wait_send()
-        for s in range(2):
-            b = 2 * j + s
-            wd[0, strip(b), :] = dot(comb[...], zs[:, column(b)]).astype(bf16)
-            put(b).start()
+        wd[0, strip(j), :] = dot(comb[...], zs[:, column(j)]).astype(bf16)
+        put(j).start()
         return 0
 
     lax.fori_loop(0, n_d, combine, 0)
-    for b in range(2 * n_d):
+    for b in range(n_d):
         put(b).wait()
 
 
@@ -323,7 +321,7 @@
         top, ff = expert.shape[3], w_gate.shape[2]
         slots = 5 * tokens * top // (4 * n_ep)
         rows = 2 * slots
-        n_d = dim // (2 * D_TILE)
+        n_d = dim // D_TILE
         units = 6 * (len(SPLITS[0]) - 1) + 1
         dma = pltpu.SemaphoreType.DMA
         hbm = pl.BlockSpec(memory_space=pltpu.MemorySpace.HBM)
@@ -336,7 +334,7 @@
             scratch_shapes=[
                 pltpu.VMEM((n_ep * slots, dim), bf16),
                 pltpu.VMEM((n_ep * slots, dim), bf16),
-                pltpu.VMEM((rows, ff), bf16),
+                pltpu.VMEM((3, rows, ff), bf16),
                 pltpu.VMEM((ff // F_TILE, dim, F_TILE), bf16),
                 pltpu.VMEM((ff // F_TILE, dim, F_TILE), bf16),
                 pltpu.VMEM((RING, ff, D_TILE), bf16),

time: 91.5 us -> 82.5 us (0.902); the launches traced: 90.3 us -> 82.4 us
  Pallas kernels: 88 us -> 80.1 us
    pallas_call x1, Pallas kernels: 88 us -> 80.1 us  [local(): pl.pallas_call(functools.partial(kernel, n_ep, slots), out_shape=jax.Shap...]
where the time goes in v2:
time: 82.5 us; the launch traced here: 82.4 us
  Pallas kernels  80.1 us (97%)
  local copies, waits for them, and re-layouts  2.3 us (3%)
    pallas_call x1, Pallas kernels, local(): pl.pallas_call(functools.partial(kernel, n_ep, slots), out_shape=jax.Shap...  80.1 us
    unnamed x1, local copies, waits for them, and re-layouts  2.3 us

profile of v2, /device:TPU:113, one launch (start us, length us, event | category | flops | bytes accessed | tf_op | source)
XLA Modules:
  0.0 82.4 jit_solution(10496974103414542429)
XLA Ops:
  0.0 80.1 %shard_map.73 = bf16[1,1,256,2048]{3,2,1,0:T(8,128)(2,1)} custom-call(bf16[1,1,256,2048]{3,2,1,0:T(8,128)(2,1)} %x_hbm.1, s32[2,256]{1,0:T(2,128)} %bitcast.9, s32[2,256]{1,0:T(2,128)} %bitcast.10, f32[2,256]{1,0:T(2,128)} %bitcast.11, bf16[1,2048,5632]{2,1,0:T(8,128)(2,1)} %wg_hbm.1, bf16[1,2048,5632]{2,1,0:T(8,128)(2,1)} %wu_hbm.1, ...), custom_call_target="tpu_custom_call" | custom-call | tf_op jit(solution)/shard_map/pallas_call | solution.py:329
  80.1 2.3 %copy.9 = bf16[1,1,256,2048]{3,2,1,0:T(8,128)(2,1)} copy(bf16[1,1,256,2048]{3,2,1,0:T(8,128)(2,1)} %shard_map.73) | data formatting | bytes 2097152

commit v3 on v2

--- a/solution.py
+++ b/solution.py
@@ -24,8 +24,8 @@
 def kernel(
     n_ep, slots,
     x_hbm, ex_ref, sl_ref, gt_ref, wg_hbm, wu_hbm, wd_hbm, y_hbm,
-    z, zs, h, wg, wu, wd, comb,
-    x_sem, g_sem, u_sem, d_sem, y_sem, out_send, out_recv, back_send, back_recv, free,
+    z, zs, h, wf, wd, comb,
+    x_sem, f_sem, d_sem, y_sem, out_send, out_recv, back_send, back_recv, free,
 ):
     tokens, dim = x_hbm.shape[2:]
     ff = h.shape[2]
@@ -44,9 +44,10 @@
 
     def load_f(i):
         cols = pl.ds(pl.multiple_of(i * F_TILE, F_TILE), F_TILE)
+        sem = f_sem.at[lax.rem(i, AHEAD)]
         return (
-            pltpu.make_async_copy(wg_hbm.at[0, :, cols], wg.at[i], g_sem.at[i]),
-            pltpu.make_async_copy(wu_hbm.at[0, :, cols], wu.at[i], u_sem.at[i]),
+            pltpu.make_async_copy(wg_hbm.at[0, :, cols], wf.at[i, 0], sem),
+            pltpu.make_async_copy(wu_hbm.at[0, :, cols], wf.at[i, 1], sem),
         )
 
     def load_d(block, slot):
@@ -61,7 +62,7 @@
 
     def get_x(b):
         return pltpu.make_async_copy(
-            x_hbm.at[0, 0, :, column(b)], wd.at[RING - 1, strip(b)], x_sem.at[b]
+            x_hbm.at[0, 0, :, column(b)], wd.at[RING - 1, strip(b)], x_sem
         )
 
     for b in range(dim // D_TILE):
@@ -92,8 +93,8 @@
         hits = [hit(p * rows, rows, k) for k in range(top)]
         any_hit = functools.reduce(jnp.logical_or, hits)
         h[0, :, p * tokens : (p + 1) * tokens] = jnp.where(any_hit, 1.0, 0.0).astype(bf16)
-    for b in range(dim // D_TILE):
-        get_x(b).wait()
+    whole = wd.at[RING - 1, pl.ds(0, dim // D_TILE * tokens)]
+    pltpu.make_async_copy(whole, whole, x_sem).wait()
 
     def dispatch(b, _):
         tile = wd[RING - 1, strip(b), :]
@@ -108,11 +109,6 @@
 
     lax.fori_loop(0, dim // D_TILE, dispatch, 0)
 
-    def unit(g, cls, c):
-        return ((g - 1) * 3 + cls) * 2 + c
-
-    last = 6 * (len(SPLITS[0]) - 1)
-
     def place(g, cls, c):
         sizes = [SPLITS[q][g] - SPLITS[q][g - 1] for q in range(3)]
         return g * rows + 2 * sum(sizes[:cls]) + c * sizes[cls], sizes[cls]
@@ -126,28 +122,24 @@
         return pltpu.make_async_remote_copy(
             src_ref=zs.at[pl.ds(home(g, cls, c), n)],
             dst_ref=z.at[pl.ds(there, n)],
-            send_sem=out_send.at[unit(g, cls, c)],
-            recv_sem=out_recv.at[unit(g, FLIP[cls], core)],
+            send_sem=out_send.at[g],
+            recv_sem=out_recv.at[g],
             device_id={"ep": peer(cls, c)},
             device_id_type=MESH,
         )
 
-    def come(g, cls, c):
-        here, n = place(g, cls, c)
-        return pltpu.make_async_remote_copy(
-            src_ref=zs.at[pl.ds(0, n)],
-            dst_ref=z.at[pl.ds(here, n)],
-            send_sem=out_send.at[unit(g, cls, c)],
-            recv_sem=out_recv.at[unit(g, cls, c)],
-            device_id={"ep": peer(cls, c)},
-            device_id_type=MESH,
+    def arrived(g):
+        to = z.at[pl.ds(g * rows, rows)]
+        return (
+            pltpu.make_async_copy(to, to, out_recv.at[g]),
+            pltpu.make_async_copy(to, to, out_send.at[g]),
         )
 
     go_sib = pltpu.make_async_remote_copy(
         src_ref=zs.at[pl.ds(slots, slots)],
         dst_ref=z.at[pl.ds(slots, slots)],
-        send_sem=out_send.at[last],
-        recv_sem=out_recv.at[last],
+        send_sem=out_send.at[0],
+        recv_sem=out_recv.at[0],
         device_id={"ep": sibling},
         device_id_type=MESH,
     )
@@ -177,21 +169,8 @@
         return pltpu.make_async_remote_copy(
             src_ref=z.at[pl.ds(here, n), cols],
             dst_ref=zs.at[pl.ds(there, n), cols],
-            send_sem=back_send.at[unit(g, cls, c), j],
-            recv_sem=back_recv.at[unit(g, FLIP[cls], core), j],
-            device_id={"ep": peer(cls, c)},
-            device_id_type=MESH,
-        )
-
-    def back_here(g, cls, c, j):
-        here = home(g, cls, c)
-        n = place(g, FLIP[cls], 0)[1]
-        cols = pl.ds(pl.multiple_of(j * wide, wide), wide)
-        return pltpu.make_async_remote_copy(
-            src_ref=z.at[pl.ds(0, n), cols],
-            dst_ref=zs.at[pl.ds(here, n), cols],
-            send_sem=back_send.at[unit(g, cls, c), j],
-            recv_sem=back_recv.at[unit(g, cls, c), j],
+            send_sem=back_send,
+            recv_sem=back_recv.at[j],
             device_id={"ep": peer(cls, c)},
             device_id_type=MESH,
         )
@@ -201,8 +180,8 @@
         return pltpu.make_async_remote_copy(
             src_ref=z.at[pl.ds(slots, slots), cols],
             dst_ref=zs.at[pl.ds(slots, slots), cols],
-            send_sem=back_send.at[last, j],
-            recv_sem=back_recv.at[last, j],
+            send_sem=back_send,
+            recv_sem=back_recv.at[j],
             device_id={"ep": sibling},
             device_id_type=MESH,
         )
@@ -211,17 +190,14 @@
         if g == 0:
             go_sib.wait()
             pl.semaphore_signal(
-                free.at[last], inc=1, device_id={"ep": sibling}, device_id_type=MESH
+                free.at[0], inc=1, device_id={"ep": sibling}, device_id_type=MESH
             )
         else:
+            for c in arrived(g):
+                c.wait()
             for cls, c in peers:
-                come(g, cls, c).wait_recv()
-                go(g, cls, c).wait_send()
                 pl.semaphore_signal(
-                    free.at[unit(g, FLIP[cls], core)],
-                    inc=1,
-                    device_id={"ep": peer(cls, c)},
-                    device_id_type=MESH,
+                    free.at[g], inc=1, device_id={"ep": peer(cls, c)}, device_id_type=MESH
                 )
 
     def expand(g, to):
@@ -229,8 +205,7 @@
 
         def gate_up(i, _):
             if g == 0:
-                for c in load_f(i):
-                    c.wait()
+                pltpu.make_async_copy(wf.at[i], wf.at[i], f_sem.at[lax.rem(i, AHEAD)]).wait()
 
                 @pl.when(i + AHEAD < n_f)
                 def _():
@@ -243,21 +218,21 @@
                     load_d(q, q).start()
 
             rows_in = z[g * rows : (g + 1) * rows, :]
-            a = dot(rows_in, wg[i])
-            b = dot(rows_in, wu[i])
+            a = dot(rows_in, wf[i, 0])
+            b = dot(rows_in, wf[i, 1])
             cols = pl.ds(pl.multiple_of(i * F_TILE, F_TILE), F_TILE)
             h[to, :, cols] = (a * jax.nn.sigmoid(a) * b).astype(bf16)
             return 0
 
-        lax.fori_loop(0, n_f, gate_up, 0)
+        if g == 0:
+            lax.fori_loop(0, n_f, gate_up, 0)
+        else:
+            for i in range(n_f):
+                gate_up(i, 0)
 
     def contract(pair, start, more):
         for g, _ in pair:
-            if g == 0:
-                pl.semaphore_wait(free.at[last], 1)
-            else:
-                for cls, c in peers:
-                    pl.semaphore_wait(free.at[unit(g, cls, c)], 1)
+            pl.semaphore_wait(free.at[g], 1 if g == 0 else len(peers))
 
         def down(j, _):
             q = start + j
@@ -295,22 +270,21 @@
 
     def put(b):
         return pltpu.make_async_copy(
-            wd.at[0, strip(b)], y_hbm.at[0, 0, :, column(b)], y_sem.at[b]
+            wd.at[0, strip(b)], y_hbm.at[0, 0, :, column(b)], y_sem
         )
 
     def combine(j, _):
-        back_sib(j).wait()
-        for g in passes:
-            for cls, c in peers:
-                back_here(g, cls, c, j).wait_recv()
-                back(g, cls, c, j).wait_send()
+        strip_in = zs.at[pl.ds(slots, (n_ep - 1) * slots), column(j)]
+        pltpu.make_async_copy(strip_in, strip_in, back_recv.at[j]).wait()
         wd[0, strip(j), :] = dot(comb[...], zs[:, column(j)]).astype(bf16)
         put(j).start()
         return 0
 
     lax.fori_loop(0, n_d, combine, 0)
-    for b in range(n_d):
-        put(b).wait()
+    sent = z.at[pl.ds(slots, (n_ep - 1) * slots)]
+    pltpu.make_async_copy(sent, sent, back_send).wait()
+    whole = wd.at[0, pl.ds(0, n_d * tokens)]
+    pltpu.make_async_copy(whole, whole, y_sem).wait()
 
 
 def solution(mesh):
@@ -322,7 +296,7 @@
         slots = 5 * tokens * top // (4 * n_ep)
         rows = 2 * slots
         n_d = dim // D_TILE
-        units = 6 * (len(SPLITS[0]) - 1) + 1
+        n_pass = len(SPLITS[0])
         dma = pltpu.SemaphoreType.DMA
         hbm = pl.BlockSpec(memory_space=pltpu.MemorySpace.HBM)
         vmem = pl.BlockSpec(memory_space=pltpu.VMEM)
@@ -335,20 +309,18 @@
                 pltpu.VMEM((n_ep * slots, dim), bf16),
                 pltpu.VMEM((n_ep * slots, dim), bf16),
                 pltpu.VMEM((3, rows, ff), bf16),
-                pltpu.VMEM((ff // F_TILE, dim, F_TILE), bf16),
-                pltpu.VMEM((ff // F_TILE, dim, F_TILE), bf16),
+                pltpu.VMEM((ff // F_TILE, 2, dim, F_TILE), bf16),
                 pltpu.VMEM((RING, ff, D_TILE), bf16),
                 pltpu.VMEM((tokens, n_ep * slots), bf16),
-                dma((dim // D_TILE,)),
-                dma((ff // F_TILE,)),
-                dma((ff // F_TILE,)),
+                dma(()),
+                dma((AHEAD,)),
                 dma((RING,)),
-                dma((dim // D_TILE,)),
-                dma((units,)),
-                dma((units,)),
-                dma((units, n_d)),
-                dma((units, n_d)),
-                pltpu.SemaphoreType.REGULAR((units,)),
+                dma(()),
+                dma((n_pass,)),
+                dma((n_pass,)),
+                dma(()),
+                dma((n_d,)),
+                pltpu.SemaphoreType.REGULAR((n_pass,)),
             ],
             compiler_params=pltpu.CompilerParams(
                 collective_id=0, has_side_effects=True, vmem_limit_bytes=67_043_328

time: 82.5 us -> 75.1 us (0.910)
  Pallas kernels: 80.1 us -> 72.6 us
    pallas_call x1, Pallas kernels: 80.1 us -> 72.6 us  [local(): pl.pallas_call(functools.partial(kernel, n_ep, slots), out_shape=jax.Shap...]
where the time goes in v3:
time: 75.1 us; the launch traced here: 74.9 us
  Pallas kernels  72.6 us (97%)
  local copies, waits for them, and re-layouts  2.3 us (3%)
    pallas_call x1, Pallas kernels, local(): pl.pallas_call(functools.partial(kernel, n_ep, slots), out_shape=jax.Shap...  72.6 us
    unnamed x1, local copies, waits for them, and re-layouts  2.3 us

profile of v3, /device:TPU:113, one launch (start us, length us, event | category | flops | bytes accessed | tf_op | source)
XLA Modules:
  0.0 74.9 jit_solution(6539077525912720510)
XLA Ops:
  0.0 72.6 %shard_map.73 = bf16[1,1,256,2048]{3,2,1,0:T(8,128)(2,1)} custom-call(bf16[1,1,256,2048]{3,2,1,0:T(8,128)(2,1)} %x_hbm.1, s32[2,256]{1,0:T(2,128)} %bitcast.9, s32[2,256]{1,0:T(2,128)} %bitcast.10, f32[2,256]{1,0:T(2,128)} %bitcast.11, bf16[1,2048,5632]{2,1,0:T(8,128)(2,1)} %wg_hbm.1, bf16[1,2048,5632]{2,1,0:T(8,128)(2,1)} %wu_hbm.1, ...), custom_call_target="tpu_custom_call" | custom-call | tf_op jit(solution)/shard_map/pallas_call | solution.py:303
  72.6 2.3 %copy.9 = bf16[1,1,256,2048]{3,2,1,0:T(8,128)(2,1)} copy(bf16[1,1,256,2048]{3,2,1,0:T(8,128)(2,1)} %shard_map.73) | data formatting | bytes 2097152

commit v4 on v3

--- a/solution.py
+++ b/solution.py
@@ -54,28 +54,25 @@
         cols = pl.ds(pl.multiple_of(block * D_TILE, D_TILE), D_TILE)
         return pltpu.make_async_copy(wd_hbm.at[0, :, cols], wd.at[slot], d_sem.at[slot])
 
-    def column(b):
-        return pl.ds(pl.multiple_of(b * D_TILE, D_TILE), D_TILE)
-
-    def strip(b):
-        return pl.ds(pl.multiple_of(b * tokens, tokens), tokens)
-
-    def get_x(b):
-        return pltpu.make_async_copy(
-            x_hbm.at[0, 0, :, column(b)], wd.at[RING - 1, strip(b)], x_sem
-        )
-
-    for b in range(dim // D_TILE):
-        get_x(b).start()
-    for i in range(AHEAD):
-        for c in load_f(i):
-            c.start()
-
     barrier = pltpu.get_barrier_semaphore()
     for k in range(1, n_ep):
         pl.semaphore_signal(
             barrier, inc=1, device_id={"ep": lax.rem(me + k, n_ep)}, device_id_type=MESH
         )
+
+    def column(b):
+        return pl.ds(pl.multiple_of(b * D_TILE, D_TILE), D_TILE)
+
+    def strip(b):
+        return pl.ds(pl.multiple_of(b * tokens, tokens), tokens)
+
+    def get_x(b):
+        return pltpu.make_async_copy(
+            x_hbm.at[0, 0, :, column(b)], wd.at[RING - 1, strip(b)], x_sem
+        )
+
+    for b in range(dim // D_TILE):
+        get_x(b).start()
 
     order = [me, sibling] + [peer(cls, c) for cls in range(3) for c in range(2)]
     top = ex_ref.shape[0]
@@ -93,21 +90,31 @@
         hits = [hit(p * rows, rows, k) for k in range(top)]
         any_hit = functools.reduce(jnp.logical_or, hits)
         h[0, :, p * tokens : (p + 1) * tokens] = jnp.where(any_hit, 1.0, 0.0).astype(bf16)
+    gates = gt_ref[...].astype(bf16).astype(f32)
+    for start in range(0, n_ep * slots, 128):
+        part = jnp.zeros((128, tokens), f32)
+        for k in range(top):
+            part = part + jnp.where(hit(start, 128, k), gates[k : k + 1, :], 0.0)
+        comb[:, start : start + 128] = part.T.astype(bf16)
+
     whole = wd.at[RING - 1, pl.ds(0, dim // D_TILE * tokens)]
     pltpu.make_async_copy(whole, whole, x_sem).wait()
-
-    def dispatch(b, _):
-        tile = wd[RING - 1, strip(b), :]
-        for p in reversed(range(n_ep // 2)):
+    for i in range(AHEAD):
+        for c in load_f(i):
+            c.start()
+
+    def dispatch(p):
+        for b in range(dim // D_TILE):
+            tile = wd[RING - 1, strip(b), :]
             out = dot(h[0, :, p * tokens : (p + 1) * tokens], tile).astype(bf16)
             if p == 0:
                 z[0:slots, column(b)] = out[0:slots]
                 zs[slots:rows, column(b)] = out[slots:rows]
             else:
                 zs[p * rows : (p + 1) * rows, column(b)] = out
-        return 0
-
-    lax.fori_loop(0, dim // D_TILE, dispatch, 0)
+
+    dispatch(2)
+    dispatch(3)
 
     def place(g, cls, c):
         sizes = [SPLITS[q][g] - SPLITS[q][g - 1] for q in range(3)]
@@ -148,17 +155,16 @@
     near = [(1, 0), (2, 0), (1, 1), (2, 1), (0, 0), (0, 1)]
 
     pl.semaphore_wait(barrier, n_ep - 1)
-    go_sib.start()
-    for g in passes:
+    for cls, c in near[:4]:
+        go(1, cls, c).start()
+    dispatch(1)
+    for cls, c in near[4:]:
+        go(1, cls, c).start()
+    for g in passes[1:]:
         for cls, c in near:
             go(g, cls, c).start()
-
-    gates = gt_ref[...].astype(bf16).astype(f32)
-    for start in range(0, n_ep * slots, 128):
-        part = jnp.zeros((128, tokens), f32)
-        for k in range(top):
-            part = part + jnp.where(hit(start, 128, k), gates[k : k + 1, :], 0.0)
-        comb[:, start : start + 128] = part.T.astype(bf16)
+    dispatch(0)
+    go_sib.start()
 
     def back(g, cls, c, j):
         here, n = place(g, cls, c)

time: 75.1 us -> 72 us (0.959)
  Pallas kernels: 72.6 us -> 69.5 us
    pallas_call x1, Pallas kernels: 72.6 us -> 69.5 us  [local(): pl.pallas_call(functools.partial(kernel, n_ep, slots), out_shape=jax.Shap...]
where the time goes in v4:
time: 72 us; the launch traced here: 71.9 us
  Pallas kernels  69.5 us (97%)
  local copies, waits for them, and re-layouts  2.3 us (3%)
    pallas_call x1, Pallas kernels, local(): pl.pallas_call(functools.partial(kernel, n_ep, slots), out_shape=jax.Shap...  69.5 us
    unnamed x1, local copies, waits for them, and re-layouts  2.3 us

profile of v4, /device:TPU:113, one launch (start us, length us, event | category | flops | bytes accessed | tf_op | source)
XLA Modules:
  0.0 71.9 jit_solution(8457589739497060652)
XLA Ops:
  0.0 69.5 %shard_map.73 = bf16[1,1,256,2048]{3,2,1,0:T(8,128)(2,1)} custom-call(bf16[1,1,256,2048]{3,2,1,0:T(8,128)(2,1)} %x_hbm.1, s32[2,256]{1,0:T(2,128)} %bitcast.9, s32[2,256]{1,0:T(2,128)} %bitcast.10, f32[2,256]{1,0:T(2,128)} %bitcast.11, bf16[1,2048,5632]{2,1,0:T(8,128)(2,1)} %wg_hbm.1, bf16[1,2048,5632]{2,1,0:T(8,128)(2,1)} %wu_hbm.1, ...), custom_call_target="tpu_custom_call" | custom-call | tf_op jit(solution)/shard_map/pallas_call | solution.py:309
  69.5 2.3 %copy.9 = bf16[1,1,256,2048]{3,2,1,0:T(8,128)(2,1)} copy(bf16[1,1,256,2048]{3,2,1,0:T(8,128)(2,1)} %shard_map.73) | data formatting | bytes 2097152

commit v5 on v4

--- a/solution.py
+++ b/solution.py
@@ -73,6 +73,9 @@
 
     for b in range(dim // D_TILE):
         get_x(b).start()
+    for i in range(AHEAD):
+        for c in load_f(i):
+            c.start(priority=1)
 
     order = [me, sibling] + [peer(cls, c) for cls in range(3) for c in range(2)]
     top = ex_ref.shape[0]
@@ -99,9 +102,6 @@
 
     whole = wd.at[RING - 1, pl.ds(0, dim // D_TILE * tokens)]
     pltpu.make_async_copy(whole, whole, x_sem).wait()
-    for i in range(AHEAD):
-        for c in load_f(i):
-            c.start()
 
     def dispatch(p):
         for b in range(dim // D_TILE):
@@ -293,6 +293,23 @@
     pltpu.make_async_copy(whole, whole, y_sem).wait()
 
 
+def carry(parts, y_in, y_out, held, in_sem, out_sem):
+    size = held.shape[0] // parts
+    ins = [
+        pltpu.make_async_copy(
+            y_in.at[0, 0, pl.ds(p * size, size)], held.at[pl.ds(p * size, size)], in_sem.at[p]
+        )
+        for p in range(parts)
+    ]
+    for c in ins:
+        c.start()
+    for p, c in enumerate(ins):
+        c.wait()
+        rows = pl.ds(p * size, size)
+        pltpu.make_async_copy(held.at[rows], y_out.at[0, 0, rows], out_sem).start()
+    pltpu.make_async_copy(held, held, out_sem).wait()
+
+
 def solution(mesh):
     n_ep = mesh.shape["ep"]
 
@@ -306,7 +323,7 @@
         dma = pltpu.SemaphoreType.DMA
         hbm = pl.BlockSpec(memory_space=pltpu.MemorySpace.HBM)
         vmem = pl.BlockSpec(memory_space=pltpu.VMEM)
-        return pl.pallas_call(
+        result = pl.pallas_call(
             functools.partial(kernel, n_ep, slots),
             out_shape=jax.ShapeDtypeStruct(x.shape, x.dtype),
             in_specs=[hbm, vmem, vmem, vmem, hbm, hbm, hbm],
@@ -340,6 +357,18 @@
             w_up,
             w_down,
         )
+        parts = 4
+        return pl.pallas_call(
+            functools.partial(carry, parts),
+            out_shape=jax.ShapeDtypeStruct(x.shape, x.dtype),
+            in_specs=[hbm],
+            out_specs=hbm,
+            scratch_shapes=[
+                pltpu.VMEM((tokens, dim), bf16),
+                dma((parts,)),
+                dma(()),
+            ],
+        )(result)
 
     act, wt = P("dp", "ep", None, None), P("ep", None, None)
     return jax.shard_map(

time: 72 us -> 71.1 us (0.987)
  local copies, waits for them, and re-layouts: 2.3 us -> 0 us
  Pallas kernels: 69.5 us -> 70.8 us
    unnamed x1 -> x0, local copies, waits for them, and re-layouts: 2.3 us -> none
    pallas_call x0 -> x1, Pallas kernels: none -> 1.95 us  [local(): pl.pallas_call(functools.partial(carry, parts), out_shape=jax.ShapeDtypeS...]
where the time goes in v5:
time: 71.1 us; the launch traced here: 71 us
  Pallas kernels  70.8 us (100%)
    pallas_call x1, Pallas kernels, local(): pl.pallas_call(functools.partial(kernel, n_ep, slots), out_shape=jax.Shap...  68.9 us
    pallas_call x1, Pallas kernels, local(): pl.pallas_call(functools.partial(carry, parts), out_shape=jax.ShapeDtypeS...  1.95 us

profile of v5, /device:TPU:113, one launch (start us, length us, event | category | flops | bytes accessed | tf_op | source)
XLA Modules:
  0.0 71.0 jit_solution(1537260938499073371)
XLA Ops:
  0.0 68.9 %shard_map.73.y_in = bf16[1,1,256,2048]{3,2,1,0:T(8,128)(2,1)} custom-call(bf16[1,1,256,2048]{3,2,1,0:T(8,128)(2,1)} %x_hbm.1, s32[2,256]{1,0:T(2,128)} %bitcast.9, s32[2,256]{1,0:T(2,128)} %bitcast.10, f32[2,256]{1,0:T(2,128)} %bitcast.11, bf16[1,2048,5632]{2,1,0:T(8,128)(2,1)} %wg_hbm.1, bf16[1,2048,5632]{2,1,0:T(8,128)(2,1)} %wu_hbm.1, ...), custom_call_target="tpu_custom_call" | custom-call | tf_op jit(solution)/shard_map/pallas_call | solution.py:326
  68.9 2.0 %shard_map.74 = bf16[1,1,256,2048]{3,2,1,0:T(8,128)(2,1)} custom-call(bf16[1,1,256,2048]{3,2,1,0:T(8,128)(2,1)} %shard_map.73.y_in), custom_call_target="tpu_custom_call" | custom-call | tf_op jit(solution)/shard_map/pallas_call | solution.py:361
